TPU v7x, 32 devices: a whole 2x2x4 slice. The times are simulated.
32 devices in a mesh: node: 4 (over z), local: 8 (over y, x, core).
Axes of the slice: x: 2, y: 2, z: 4, core: 2. Of those that a mesh axis runs over, the one named last changes fastest.
Arguments:
- tokens: bfloat16 [4096, 5120], P(('node', 'local')), may hold values from -6 to 6
- routes: int32 [4096, 6], P(('node', 'local')), may hold values from 0 to 31, all different within a row; in each aligned block of 128 rows (0 to 127, 128 to 255, ...) at most 32 rows name the same one
- route_weights: float32 [4096, 6], P(('node', 'local')), may hold values from 0.05 to 1
- w_gate: bfloat16 [32, 5120, 768], P(('node', 'local')), may hold values from -0.078125 to 0.078125
- w_up: bfloat16 [32, 5120, 768], P(('node', 'local')), may hold values from -0.078125 to 0.078125
- w_down: bfloat16 [32, 768, 5120], P(('node', 'local')), may hold values from -0.21875 to 0.21875
Outputs:
- mixed: bfloat16 [4096, 5120], P(('node', 'local'))
- balance_loss: float32 [], replicated
Inputs may be any that keep to these rules, and one draw needn't show every extreme that they name: `routes`: each row names 6 different experts. Among the rows of one device no expert is named more than 32 times, a bound that some block reaches.
All inputs are finite; a program needn't handle non-finite values.
Results may differ from a plain program's by a relative error of at most 0.0025.
The roundings to bfloat16 on the way count: a program that leaves them out, or rounds other values in their place, can miss the bound.
Values may be sent and summed in bfloat16 or wider, within the bound.
A program may use at most 128 MiB of HBM per device.

v0:
```python
import jax
import jax.numpy as jnp
from jax import lax
from jax.sharding import PartitionSpec as P

TOPK = 6


def expert_apply(rows, w_gate, w_up, w_down):
    gate = jnp.einsum("erd,edf->erf", rows, w_gate, preferred_element_type=jnp.float32)
    upper = jnp.einsum("erd,edf->erf", rows, w_up, preferred_element_type=jnp.float32)
    hidden = (jax.nn.silu(gate) * upper).astype(jnp.bfloat16)
    return jnp.einsum("erf,efd->erd", hidden, w_down, preferred_element_type=jnp.float32).astype(
        jnp.bfloat16
    )


def local(tokens, routes, route_weights, w_gate, w_up, w_down):
    n_node = lax.axis_size("node")
    n_local = lax.axis_size("local")
    exp_dev = w_gate.shape[0]
    devices = n_node * n_local
    experts = exp_dev * devices
    tok_dev = tokens.shape[0]
    width = tokens.shape[1]
    capacity = 4 * tok_dev * TOPK // (3 * experts)
    flat = routes.reshape(-1)
    labels = jnp.arange(experts, dtype=jnp.int32)
    onehot = (flat[:, None] == labels[None, :]).astype(jnp.int32)
    running = jnp.cumsum(onehot, axis=0) - onehot
    slots = jnp.sum(running * onehot, axis=1)
    position = flat * capacity + slots
    counts = jnp.sum(onehot, axis=0).astype(jnp.float32)
    weight_sums = jnp.sum(onehot.astype(jnp.float32) * route_weights.reshape(-1)[:, None], axis=0)
    counts_all, sums_all = lax.psum((counts, weight_sums), ("node", "local"))
    repeated = jnp.repeat(tokens, TOPK, axis=0)
    outgoing = jnp.zeros((experts * capacity, width), jnp.bfloat16).at[position].set(repeated)
    piece = lax.all_to_all(
        outgoing.reshape(experts, 1, capacity, width),
        ("node", "local"),
        split_axis=0,
        concat_axis=1,
        tiled=True,
    )
    held, sources, count, breadth = piece.shape
    rows = piece.reshape(held, sources * count, breadth)
    result = expert_apply(rows, w_gate, w_up, w_down)
    result = result.reshape(held, sources, count, breadth)
    returned = lax.all_to_all(result, ("node", "local"), split_axis=1, concat_axis=0, tiled=True)
    returned = returned.reshape(experts * capacity, width)
    picked = returned[position].reshape(tok_dev, TOPK, width).astype(jnp.float32)
    mixed = jnp.sum(route_weights[:, :, None] * picked, axis=1).astype(jnp.bfloat16)
    total = jnp.float32(tok_dev * devices)
    balance_loss = (
        jnp.sum(counts_all * sums_all) * jnp.float32(experts) / (jnp.float32(TOPK) * total * total)
    )
    return (mixed, balance_loss)


def solution(mesh):
    placed = (
        P(("node", "local"), None),
        P(("node", "local"), None),
        P(("node", "local"), None),
        P(("node", "local"), None, None),
        P(("node", "local"), None, None),
        P(("node", "local"), None, None),
    )
    return jax.shard_map(
        local,
        mesh=mesh,
        in_specs=placed,
        out_specs=(P(("node", "local"), None), P()),
        check_vma=False,
    )
```

profile of v0, /device:TPU:0, one launch (start us, length us, event | category | flops | bytes accessed | tf_op | source)
XLA Modules:
  0.0 619.0 jit_solution(2982418131425307916)
XLA Ops:
  0.6 0.8 copy.17
  1.4 0.1 eq.29
  1.6 0.1 eq.25
  1.7 0.7 broadcast_multiply_fusion
  2.4 1.7 reduce-window.6
  4.1 0.3 slice_reduce_fusion
  4.4 0.1 copy.16
  4.5 0.1 mul.53
  4.7 6.3 %broadcast_in_dim.5 = bf16[128,6,5120]{2,1,0:T(8,128)(2,1)} broadcast(bf16[128,5120]{1,0:T(8,128)(2,1)} %param.6), dimensions={0,2} | broadcast | bytes 9175040 | tf_op jit(solution)/shard_map/broadcast_in_dim | solution.py:36
  11.0 13.2 %reshape.127 = bf16[768,5120]{1,0:T(8,128)(2,1)} reshape(bf16[128,6,5120]{2,1,0:T(8,128)(2,1)} %broadcast_in_dim.5) | data formatting | bytes 15728640 | tf_op jit(solution)/shard_map/reshape | solution.py:36
  24.2 0.1 convert_reduce_fusion
  24.4 21.7 %scatter_custom_fusion = bf16[1024,5120]{1,0:T(8,128)(2,1)} fusion(s32[768]{0:T(1024)S(1)} %fusion.14, bf16[768,5120]{1,0:T(8,128)(2,1)} %reshape.127, bf16[]{:T(256)} %constant.7.clone.1), kind=kCustom, calls=%fused_computation.9 | custom fusion | bytes 10486272 | tf_op jit(solution)/shard_map/scatter | solution.py:37
  46.1 0.0 slice-start
  46.1 235.8 %all_to_all.8 = bf16[32,1,32,5120]{3,2,1,0:T(8,128)(2,1)S(1)} all-to-all(bf16[32,1,32,5120]{3,2,1,0:T(8,128)(2,1)} %bitcast.32), channel_id=1, replica_groups=mesh['node'=4,'local'=8] {'node','local'}, dimensions={0} | all-to-all | bytes 20971520 | tf_op jit(solution)/shard_map/all_to_all | solution.py:38
  281.9 0.0 slice-start.1
  281.9 10.9 %fusion.1 = f32[1024,768]{1,0:T(8,128)S(1)} fusion(bf16[1024,5120]{1,0:T(8,128)(2,1)S(1)} %bitcast.34, bf16[1,5120,768]{2,1,0:T(8,128)(2,1)} %param.10), kind=kOutput, calls=%fused_computation.5 | convolution fusion | flops 8053063680 | bytes 21495808 | tf_op jit(solution)/shard_map/erd,edf->erf/dot_general | solution.py:11
  292.8 0.0 slice-done
  292.8 0.0 slice-done.1
  292.8 8.6 %multiply_convert_fusion = bf16[1024,768]{1,0:T(8,128)(2,1)S(1)} fusion(f32[1024,768]{1,0:T(8,128)S(1)} %fusion.1, bf16[1024,5120]{1,0:T(8,128)(2,1)S(1)} %bitcast.35, bf16[1,5120,768]{2,1,0:T(8,128)(2,1)S(1)} %bitcast.38), kind=kOutput, calls=%fused_computation.11 | convolution fusion | flops 8057782272 | bytes 23068672 | tf_op jit(solution)/shard_map/erd,edf->erf/dot_general | solution.py:10
  301.4 13.7 %convolution_convert_fusion = bf16[1024,5120]{1,0:T(8,128)(2,1)} fusion(bf16[1024,768]{1,0:T(8,128)(2,1)S(1)} %multiply_convert_fusion, bf16[1,768,5120]{2,1,0:T(8,128)(2,1)} %param.11), kind=kOutput, calls=%fused_computation.3 | convolution fusion | flops 8058306560 | bytes 19922944 | tf_op jit(solution)/shard_map/erf,efd->erd/dot_general | solution.py:13
  315.1 0.0 copy-start
  315.1 3.9 all-to-all-start.1
  319.0 0.0 copy-done
  319.0 0.1 copy.15
  319.1 0.1 mul.58
  319.3 0.1 fusion.12
  319.4 250.9 %all-reduce = (f32[32]{0:T(128)S(1)}, f32[32]{0:T(128)S(1)}) all-reduce(f32[32]{0:T(128)S(1)} %convert_element_type.37, f32[32]{0:T(128)S(1)} %fusion.12), channel_id=1, replica_groups=mesh['node'=4,'local'=8] {'node','local'}, use_global_device_ids=true, to_apply=%region_6.7 | all-reduce | flops 64 | bytes 512 | tf_op jit(solution)/shard_map/psum | solution.py:35
  570.3 0.6 multiply_reduce_fusion.1
  571.6 0.0 all-to-all-done.1
  571.6 20.0 %gather_fusion = bf16[768,5120]{1,0:T(8,128)(2,1)} fusion(bf16[1024,5120]{1,0:T(8,128)(2,1)} %bitcast.8, s32[1024]{0:T(1024)S(1)} %pad_clamp_fusion), kind=kCustom, calls=%fused_computation | custom fusion | bytes 15731712 | tf_op jit(solution)/shard_map/gather | solution.py:51
  591.6 14.3 %reshape.114 = f32[128,6,5120]{2,1,0:T(8,128)} reshape(bf16[768,5120]{1,0:T(8,128)(2,1)} %gather_fusion) | data formatting | bytes 23592960 | tf_op jit(solution)/shard_map/convert_element_type | solution.py:51
  605.9 12.0 %multiply_reduce_fusion = bf16[128,5120]{1,0:T(8,128)(2,1)} fusion(f32[128,6,5120]{2,1,0:T(8,128)} %reshape.114, f32[128,6]{1,0:T(8,128)S(1)} %copy.15), kind=kLoop, calls=%fused_computation.2 | loop fusion | flops 7208960 | bytes 17042432 | tf_op jit(solution)/shard_map/reduce_sum | solution.py:52
  (6 shorter events, 0.1 us)
Async XLA Ops:
  46.1 246.7 %slice-start = ((s8[7864320]{0:T(1024)(128)(4,1)}), s8[4194304]{0:T(1024)(128)(4,1)S(1)}, s32[]{:S(2)}) async-start(s8[7864320]{0:T(1024)(128)(4,1)} %bitcast.37), calls=%async_computation.2 | async-start | bytes 8388608
  281.9 10.9 %slice-start.1 = ((s8[7864320]{0:T(1024)(128)(4,1)}), s8[3670016]{0:T(1024)(128)(4,1)S(1)}, s32[]{:S(2)}) async-start(s8[7864320]{0:T(1024)(128)(4,1)} %bitcast.37), calls=%async_computation.3 | async-start | bytes 7340032
  315.1 3.9 copy-start
  315.1 256.4 %all-to-all-start.1 = ((bf16[1,32,32,5120]{3,2,0,1:T(8,128)(2,1)}), bf16[1,32,32,5120]{3,2,0,1:T(8,128)(2,1)}, u32[]{:S(2)}, u32[]{:S(2)}) async-start(bf16[1,32,32,5120]{3,2,0,1:T(8,128)(2,1)} %bitcast.33), calls=%async_computation.1 | async-start | bytes 20971520 | tf_op jit(solution)/shard_map/all_to_all | solution.py:49
where the time goes:
time: 620 us; the launch traced here: 619 us
  blocking collectives  487 us (79%)
  local copies, waits for them, and re-layouts  77.4 us (12%)
  matrix products  33.2 us (5%)
  other arithmetic  15.4 us (2%)
    psum x1, blocking collectives, local(): counts_all, sums_all = lax.psum((counts, weight_sums), ('node', 'local'))  251 us
    all_to_all x1, blocking collectives, local(): lax.all_to_all(outgoing.reshape(experts, 1, capacity, width), ('node', 'l...  236 us
    scatter x1, local copies, waits for them, and re-layouts, local(): jnp.zeros((experts * capacity, width), jnp.bfloat16).at[position]  21.7 us
    gather x1, local copies, waits for them, and re-layouts, local(): returned[position].reshape(tok_dev, TOPK, width).astype(jnp.float32)  20 us
    convert_element_type x1, local copies, waits for them, and re-layouts, local(): returned[position].reshape(tok_dev, TOPK, width).astype(jnp.float32)  14.3 us
    dot_general x1, matrix products, expert_apply(): jnp.einsum('erf,efd->erd', hidden, w_down, preferred_element_type=jnp.flo...  13.7 us
    reshape x1, local copies, waits for them, and re-layouts, local(): repeated = jnp.repeat(tokens, TOPK, axis=0)  13.2 us
  transfers between devices with their start and end apart: 1, of which 0 were waited for; matrix products, arithmetic and copies ran while one was open for 0% of the time, Pallas kernels for 0%

commit v1 on v0

--- a/solution.py
+++ b/solution.py
@@ -35,12 +35,20 @@
     counts_all, sums_all = lax.psum((counts, weight_sums), ("node", "local"))
     repeated = jnp.repeat(tokens, TOPK, axis=0)
     outgoing = jnp.zeros((experts * capacity, width), jnp.bfloat16).at[position].set(repeated)
-    piece = lax.all_to_all(
-        outgoing.reshape(experts, 1, capacity, width),
-        ("node", "local"),
-        split_axis=0,
-        concat_axis=1,
-        tiled=True,
+    piece = jnp.concatenate(
+        lax.all_to_all(
+            jnp.stack(
+                jnp.split(
+                    outgoing.reshape(experts, 1, capacity, width),
+                    lax.axis_size(("node", "local")),
+                    axis=0,
+                )
+            ),
+            ("node", "local"),
+            0,
+            0,
+        ),
+        axis=1,
     )
     held, sources, count, breadth = piece.shape
     rows = piece.reshape(held, sources * count, breadth)

time: 620 us -> 650 us (1.048)
  local copies, waits for them, and re-layouts: 77.4 us -> 110 us
    unnamed x8 -> x43, local copies, waits for them, and re-layouts: 0.92 us -> 32 us
where the time goes in v1:
time: 650 us; the launch traced here: 648 us
  blocking collectives  486 us (75%)
  local copies, waits for them, and re-layouts  110 us (17%)
  matrix products  29.7 us (5%)
  other arithmetic  15.4 us (2%)
    psum x1, blocking collectives, local(): counts_all, sums_all = lax.psum((counts, weight_sums), ('node', 'local'))  251 us
    all_to_all x1, blocking collectives, local(): lax.all_to_all(jnp.stack(jnp.split(outgoing.reshape(experts, 1, capacity,...  236 us
    unnamed x43, local copies, waits for them, and re-layouts  32 us
    scatter x1, local copies, waits for them, and re-layouts, local(): jnp.zeros((experts * capacity, width), jnp.bfloat16).at[position]  21.7 us
    gather x1, local copies, waits for them, and re-layouts, local(): returned[position].reshape(tok_dev, TOPK, width).astype(jnp.float32)  20 us
    convert_element_type x1, local copies, waits for them, and re-layouts, local(): returned[position].reshape(tok_dev, TOPK, width).astype(jnp.float32)  14.3 us
    reshape x1, local copies, waits for them, and re-layouts, local(): repeated = jnp.repeat(tokens, TOPK, axis=0)  13.2 us
  transfers between devices with their start and end apart: 1, of which 0 were waited for; matrix products, arithmetic and copies ran while one was open for 0% of the time, Pallas kernels for 0%

profile of v1, /device:TPU:0, one launch (start us, length us, event | category | flops | bytes accessed | tf_op | source)
XLA Modules:
  0.0 647.8 jit_solution(13282105609958515353)
XLA Ops:
  0.6 0.8 copy.17
  1.4 0.1 eq.29
  1.6 0.1 eq.25
  1.7 0.7 broadcast_multiply_fusion
  2.4 1.7 reduce-window.6
  4.1 0.3 slice_reduce_fusion
  4.4 0.1 copy.16
  4.5 0.1 mul.53
  4.7 6.3 broadcast_in_dim.5
  11.0 13.2 %reshape.183 = bf16[768,5120]{1,0:T(8,128)(2,1)} reshape(bf16[128,6,5120]{2,1,0:T(8,128)(2,1)} %broadcast_in_dim.5) | data formatting | bytes 15728640 | tf_op jit(solution)/shard_map/reshape | solution.py:36
  24.2 0.1 convert_reduce_fusion
  24.4 21.7 %scatter_custom_fusion = bf16[1024,5120]{1,0:T(8,128)(2,1)} fusion(s32[768]{0:T(1024)S(1)} %fusion.46, bf16[768,5120]{1,0:T(8,128)(2,1)} %reshape.183, bf16[]{:T(256)} %constant.7.clone.1), kind=kCustom, calls=%fused_computation.9 | custom fusion | bytes 10486272 | tf_op jit(solution)/shard_map/scatter | solution.py:37
  46.1 1.0 fusion.40
  47.1 1.0 fusion.39
  48.1 1.0 fusion.38
  49.1 1.0 fusion.37
  50.1 1.0 fusion.36
  51.1 1.0 fusion.35
  52.1 1.0 fusion.34
  53.1 1.0 fusion.33
  54.1 1.0 fusion.32
  55.1 1.0 fusion.31
  56.1 1.0 fusion.30
  57.1 1.0 fusion.29
  58.1 1.0 fusion.28
  59.1 1.0 fusion.27
  60.1 1.0 fusion.26
  61.1 1.0 fusion.25
  62.1 1.0 fusion.24
  63.1 1.0 fusion.23
  64.1 1.0 fusion.22
  65.1 1.0 fusion.21
  66.1 1.0 fusion.20
  67.1 1.0 fusion.19
  68.1 1.0 fusion.18
  69.1 1.0 fusion.17
  70.1 1.0 fusion.16
  71.1 1.0 fusion.15
  72.1 1.0 fusion.14
  73.1 1.0 fusion.13
  74.1 1.0 fusion.12
  75.1 1.0 fusion.11
  76.1 0.0 slice-start
  76.1 1.1 fusion.10
  77.3 1.2 fusion.9
  78.5 0.0 slice-start.1
  78.5 235.6 %all_to_all.14 = bf16[32,1,1,32,5120]{4,3,2,1,0:T(8,128)(2,1)S(1)} all-to-all(bf16[32,1,1,32,5120]{4,3,2,1,0:T(8,128)(2,1)S(1)} %fusion.9), channel_id=1, replica_groups=mesh['node'=4,'local'=8] {'node','local'}, dimensions={0} | all-to-all | bytes 20971520 | tf_op jit(solution)/shard_map/all_to_all | solution.py:39
  314.0 0.0 slice-done
  314.0 0.0 slice-done.1
  314.1 8.3 %fusion.1 = f32[1024,768]{1,0:T(8,128)S(1)} fusion(bf16[1024,5120]{1,0:T(8,128)(2,1)S(1)} %bitcast.160, bf16[1,5120,768]{2,1,0:T(8,128)(2,1)S(1)} %bitcast.164), kind=kOutput, calls=%fused_computation.5 | convolution fusion | flops 8053063680 | bytes 21495808 | tf_op jit(solution)/shard_map/erd,edf->erf/dot_general | solution.py:11
  322.3 0.0 slice-start.3
  322.4 10.7 %multiply_convert_fusion = bf16[1024,768]{1,0:T(8,128)(2,1)S(1)} fusion(f32[1024,768]{1,0:T(8,128)S(1)} %fusion.1, bf16[1024,5120]{1,0:T(8,128)(2,1)S(1)} %bitcast.161, bf16[1,5120,768]{2,1,0:T(8,128)(2,1)} %param.9), kind=kOutput, calls=%fused_computation.11 | convolution fusion | flops 8057782272 | bytes 23068672 | tf_op jit(solution)/shard_map/erd,edf->erf/dot_general | solution.py:10
  333.1 0.0 slice-done.2
  333.1 10.7 %convolution_convert_fusion = bf16[1024,5120]{1,0:T(8,128)(2,1)} fusion(bf16[1024,768]{1,0:T(8,128)(2,1)S(1)} %multiply_convert_fusion, bf16[1,768,5120]{2,1,0:T(8,128)(2,1)S(1)} %bitcast.166), kind=kOutput, calls=%fused_computation.3 | convolution fusion | flops 8058306560 | bytes 19922944 | tf_op jit(solution)/shard_map/erf,efd->erd/dot_general | solution.py:13
  343.9 3.9 all-to-all-start.1
  347.7 0.1 copy.15
  347.9 0.1 mul.58
  348.0 0.1 fusion.44
  348.1 250.9 %all-reduce = (f32[32]{0:T(128)S(1)}, f32[32]{0:T(128)S(1)}) all-reduce(f32[32]{0:T(128)S(1)} %convert_element_type.37, f32[32]{0:T(128)S(1)} %fusion.44), channel_id=1, replica_groups=mesh['node'=4,'local'=8] {'node','local'}, use_global_device_ids=true, to_apply=%region_6.7 | all-reduce | flops 64 | bytes 512 | tf_op jit(solution)/shard_map/psum | solution.py:35
  599.0 0.6 multiply_reduce_fusion.1
  600.3 0.0 all-to-all-done.1
  600.3 20.0 %gather_fusion = bf16[768,5120]{1,0:T(8,128)(2,1)} fusion(bf16[1024,5120]{1,0:T(8,128)(2,1)} %bitcast.39, s32[1024]{0:T(1024)S(1)} %pad_clamp_fusion), kind=kCustom, calls=%fused_computation | custom fusion | bytes 15731712 | tf_op jit(solution)/shard_map/gather | solution.py:59
  620.3 14.3 %reshape.170 = f32[128,6,5120]{2,1,0:T(8,128)} reshape(bf16[768,5120]{1,0:T(8,128)(2,1)} %gather_fusion) | data formatting | bytes 23592960 | tf_op jit(solution)/shard_map/convert_element_type | solution.py:59
  634.6 12.0 %multiply_reduce_fusion = bf16[128,5120]{1,0:T(8,128)(2,1)} fusion(f32[128,6,5120]{2,1,0:T(8,128)} %reshape.170, f32[128,6]{1,0:T(8,128)S(1)} %copy.15), kind=kLoop, calls=%fused_computation.2 | loop fusion | flops 7208960 | bytes 17042432 | tf_op jit(solution)/shard_map/reduce_sum | solution.py:60
  (11 shorter events, 0.1 us)
Async XLA Ops:
  76.1 238.0 %slice-start = ((s8[7864320]{0:T(1024)(128)(4,1)}), s8[4194304]{0:T(1024)(128)(4,1)S(1)}, s32[]{:S(2)}) async-start(s8[7864320]{0:T(1024)(128)(4,1)} %bitcast.163), calls=%async_computation.2 | async-start | bytes 8388608
  78.5 235.6 %slice-start.1 = ((s8[7864320]{0:T(1024)(128)(4,1)}), s8[3670016]{0:T(1024)(128)(4,1)S(1)}, s32[]{:S(2)}) async-start(s8[7864320]{0:T(1024)(128)(4,1)} %bitcast.163), calls=%async_computation.3 | async-start | bytes 7340032
  314.1 19.1 %slice-start.2 = ((s8[7864320]{0:T(1024)(128)(4,1)}), s8[3670016]{0:T(1024)(128)(4,1)S(1)}, s32[]{:S(2)}) async-start(s8[7864320]{0:T(1024)(128)(4,1)} %bitcast.165), calls=%async_computation.4 | async-start | bytes 7340032
  322.3 10.8 %slice-start.3 = ((s8[7864320]{0:T(1024)(128)(4,1)}), s8[4194304]{0:T(1024)(128)(4,1)S(1)}, s32[]{:S(2)}) async-start(s8[7864320]{0:T(1024)(128)(4,1)} %bitcast.165), calls=%async_computation.5 | async-start | bytes 8388608
  343.9 3.9 copy-start
  343.9 256.4 %all-to-all-start.1 = ((bf16[1,32,32,5120]{3,2,0,1:T(8,128)(2,1)}), bf16[1,32,32,5120]{3,2,0,1:T(8,128)(2,1)}, u32[]{:S(2)}, u32[]{:S(2)}) async-start(bf16[1,32,32,5120]{3,2,0,1:T(8,128)(2,1)} %bitcast.159), calls=%async_computation.1 | async-start | bytes 20971520 | tf_op jit(solution)/shard_map/all_to_all | solution.py:57
